TPU v7x, 1024 devices: a whole 4x8x16 slice. The times are simulated.
1024 devices in a mesh: gx: 8 (over z_lo), gy: 16 (over y, z_hi), gz: 8 (over x, core).
Axes of the slice: x: 4, y: 8, z: 16 (z_hi: 2, z_lo: 8; z = z_hi * 8 + z_lo), core: 2. Of those that a mesh axis runs over, the one named last changes fastest.
Arguments:
- coefficients: bfloat16 [64, 256, 128, 128], P('gx', 'gy', 'gz'), may hold values from -0.109375 to 0.109375
- potential: float32 [64, 256, 128], P('gx', 'gy', 'gz'), may hold values from 0.5 to 2
- owner_map: int32 [8, 16, 8, 7, 1], P('gx', 'gy', 'gz'), may hold values from 0 to 7; in each aligned block of 7 rows (0 to 6, 7 to 13, ..., all dimensions but the last counted through in order) at most 2 rows name the same one
Outputs:
- correction: bfloat16 [8, 16, 8, 16, 128, 128], P('gx', 'gy', 'gz')
Inputs may be any that keep to these rules, and one draw needn't show every extreme that they name: `owner_map`: among the 7 blocks of one subdomain no owner is named more than 2 times; in every draw some subdomain names some owner exactly 2 times.
All inputs are finite; a program needn't handle non-finite values.
Results may differ from a plain program's by a relative error of at most 0.0062.
Values may be sent and summed in bfloat16 or wider, within the bound.
A program may use at most 32 MiB of HBM per device.

v0:
```python
import math

import jax
import jax.numpy as jnp
from jax import lax
from jax.sharding import PartitionSpec as P

CAP = 2


SMOOTH = 0.25


def with_halo(array, sides, width):
    edges = {}
    for axis, dim in sides:
        count, length = (lax.axis_size(axis), array.shape[dim])
        up = [(i, (i + 1) % count) for i in range(count)]
        last = lax.slice_in_dim(array, length - width, length, axis=dim)
        first = lax.slice_in_dim(array, 0, width, axis=dim)
        edges[dim] = (
            lax.ppermute(last, axis, up),
            lax.ppermute(first, axis, [(b, a) for a, b in up]),
        )
    done = []
    for _, dim in sides:
        low, high = edges[dim]
        around = [(width, width) if d in done else (0, 0) for d in range(array.ndim)]
        array = jnp.concatenate([jnp.pad(low, around), array, jnp.pad(high, around)], axis=dim)
        done.append(dim)
    return array


def moved(field, dim, step):
    count = field.shape[dim]
    zero = jnp.zeros_like(lax.slice_in_dim(field, 0, 1, axis=dim))
    if step > 0:
        return jnp.concatenate([lax.slice_in_dim(field, 1, count, axis=dim), zero], axis=dim)
    return jnp.concatenate([zero, lax.slice_in_dim(field, 0, count - 1, axis=dim)], axis=dim)


def neighbour_sum(field, dims):
    total = jnp.zeros(field.shape, jnp.float32)
    for dim in dims:
        total = (
            total
            + moved(field, dim, 1).astype(jnp.float32)
            + moved(field, dim, -1).astype(jnp.float32)
        )
    return total


def gram(left, right):
    width = left.shape[-1]
    return jnp.dot(
        left.reshape(-1, width).T,
        right.reshape(-1, right.shape[-1]),
        preferred_element_type=jnp.float32,
    )


def layer(field, dim, where):
    return lax.slice_in_dim(field, where, where + 1, axis=dim)


def local(coefficients, potential, owner_map):
    cells = coefficients.shape[:3]
    orbitals = coefficients.shape[3]
    smooth = (
        coefficients.astype(jnp.float32) + SMOOTH * neighbour_sum(coefficients, (0, 1, 2))
    ).astype(jnp.bfloat16)
    weighted = (potential[..., None] * smooth.astype(jnp.float32)).astype(jnp.bfloat16)
    hamilton = gram(smooth, weighted).astype(jnp.bfloat16)
    correlation = gram(smooth, smooth)
    faces = []
    padded = with_halo(coefficients, (("gx", 0), ("gy", 1), ("gz", 2)), 2)
    for dim in range(3):
        lateral = tuple((other for other in range(3) if other != dim))
        size = cells[dim]
        for side in (-1, 1):
            edge = 0 if side < 0 else size - 1
            c_own = layer(coefficients, dim, edge)
            s_own = layer(smooth, dim, edge)
            far_at = 1 if side < 0 else size + 2
            deep_at = 0 if side < 0 else size + 3
            slab = lax.slice_in_dim(
                padded, min(far_at, deep_at), min(far_at, deep_at) + 2, axis=dim
            )
            for other in lateral:
                slab = lax.slice_in_dim(slab, 2, 2 + cells[other], axis=other)
            far_local = far_at - min(far_at, deep_at)
            deep_local = deep_at - min(far_at, deep_at)
            c_far = layer(slab, dim, far_local)
            c_deep = layer(slab, dim, deep_local)
            s_far = (
                c_far.astype(jnp.float32)
                + SMOOTH * (c_deep.astype(jnp.float32) + neighbour_sum(c_far, lateral))
            ).astype(jnp.bfloat16)
            correlation = correlation + SMOOTH * SMOOTH * gram(c_own, c_own)
            faces.append(SMOOTH * (gram(s_own, c_far) + gram(c_own, s_far)))
    scale = jnp.float32(math.sqrt(cells[0] * cells[1] * cells[2]))
    blocks = jnp.stack([correlation - jnp.eye(orbitals, dtype=jnp.float32)] + faces)
    deviation = (scale * blocks).astype(jnp.bfloat16)
    count = deviation.shape[0]
    routes = owner_map.reshape(count)
    order = jnp.arange(count, dtype=jnp.int32)
    same = routes[:, None] == routes[None, :]
    earlier = order[None, :] < order[:, None]
    rank = jnp.sum((same & earlier).astype(jnp.int32), axis=1)
    owners = lax.axis_size("gx")
    target = (routes[None, None, :] == jnp.arange(owners, dtype=jnp.int32)[:, None, None]) & (
        rank[None, None, :] == jnp.arange(CAP, dtype=jnp.int32)[None, :, None]
    )
    pick = target.astype(jnp.bfloat16)
    product = jnp.einsum(
        "fab,bc->fac", deviation, hamilton, preferred_element_type=jnp.float32
    ).astype(jnp.bfloat16)
    chosen = jnp.einsum("osf,fab->osab", pick, product, preferred_element_type=jnp.float32).astype(
        jnp.bfloat16
    )
    result = lax.all_to_all(chosen, "gx", split_axis=0, concat_axis=0, tiled=True)
    return result.reshape(1, 1, 1, owners * CAP, orbitals, orbitals)


def solution(mesh):
    in_specs = (P("gx", "gy", "gz", None), P("gx", "gy", "gz"), P("gx", "gy", "gz", None, None))
    out_specs = P("gx", "gy", "gz", None, None, None)
    return jax.shard_map(local, mesh=mesh, in_specs=in_specs, out_specs=out_specs, check_vma=False)
```

profile of v0, /device:TPU:7, one launch (start us, length us, event | category | flops | bytes accessed | tf_op | source)
XLA Modules:
  0.0 87.1 jit_solution(12706482162012993171)
XLA Ops:
  0.0 0.0 copy-start
  0.0 1.0 %fusion.153 = (bf16[2,16,16,128]{3,2,1,0:T(8,128)(2,1)S(1)}, bf16[2,16,16,128]{3,2,1,0:T(8,128)(2,1)S(1)}) fusion(bf16[8,16,16,128]{3,2,1,0:T(8,128)(2,1)} %param.3), kind=kLoop, calls=%fused_computation.188 | loop fusion | bytes 524288 | tf_op jit(solution)/shard_map/slice | solution.py:20
  1.0 4.0 %collective-permute-start = (bf16[2,16,16,128]{3,2,1,0:T(8,128)(2,1)S(1)}, bf16[2,16,16,128]{3,2,1,0:T(8,128)(2,1)S(1)}, u32[]{:S(2)}, u32[]{:S(2)}) collective-permute-start(bf16[2,16,16,128]{3,2,1,0:T(8,128)(2,1)S(1)} %get-tuple-element.12), channel_id=1, source_target_pairs={{0,128},{128,256},{256,384},{384,512},{512,640},{640,768},{768,896... | collective-permute-start | bytes 393224 | tf_op jit(solution)/shard_map/ppermute | solution.py:22
  5.1 14.0 %collective-permute-start.1 = (bf16[2,16,16,128]{3,2,1,0:T(8,128)(2,1)S(1)}, bf16[2,16,16,128]{3,2,1,0:T(8,128)(2,1)S(1)}, u32[]{:S(2)}, u32[]{:S(2)}) collective-permute-start(bf16[2,16,16,128]{3,2,1,0:T(8,128)(2,1)S(1)} %get-tuple-element.11), channel_id=1, source_target_pairs={{128,0},{256,128},{384,256},{512,384},{640,512},{768,640},{896,768... | collective-permute-start | bytes 393224 | tf_op jit(solution)/shard_map/ppermute | solution.py:23
  19.0 0.0 copy-done
  19.1 13.0 %collective-permute-start.2 = (bf16[8,2,16,128]{3,2,0,1:T(8,128)(2,1)S(1)}, bf16[8,2,16,128]{3,2,0,1:T(8,128)(2,1)S(1)}, u32[]{:S(2)}, u32[]{:S(2)}) collective-permute-start(bf16[8,2,16,128]{3,2,0,1:T(8,128)(2,1)S(1)} %copy.86), channel_id=1, source_target_pairs={{0,8},{8,16},{16,24},{24,32},{32,40},{40,48},{48,56},{56,64},{64,7... | collective-permute-start | bytes 196616 | tf_op jit(solution)/shard_map/ppermute | solution.py:22
  32.1 4.8 %collective-permute-start.3 = (bf16[8,2,16,128]{3,2,0,1:T(8,128)(2,1)S(1)}, bf16[8,2,16,128]{3,2,0,1:T(8,128)(2,1)S(1)}, u32[]{:S(2)}, u32[]{:S(2)}) collective-permute-start(bf16[8,2,16,128]{3,2,0,1:T(8,128)(2,1)S(1)} %copy.87), channel_id=1, source_target_pairs={{8,0},{16,8},{24,16},{32,24},{40,32},{48,40},{56,48},{64,56},{72,6... | collective-permute-start | bytes 196616 | tf_op jit(solution)/shard_map/ppermute | solution.py:23
  36.9 0.1 fusion.151
  37.1 6.7 %collective-permute-start.4 = (bf16[8,16,2,128]{3,1,0,2:T(8,128)(2,1)S(1)}, bf16[8,16,2,128]{3,1,0,2:T(8,128)(2,1)S(1)}, u32[]{:S(2)}, u32[]{:S(2)}) collective-permute-start(bf16[8,16,2,128]{3,1,0,2:T(8,128)(2,1)S(1)} %copy.88), channel_id=1, source_target_pairs={{0,1},{1,2},{2,3},{3,4},{4,5},{5,6},{6,7},{7,0},{8,9},{9,10},{10,1... | collective-permute-start | bytes 196616 | tf_op jit(solution)/shard_map/ppermute | solution.py:22
  43.8 0.2 fusion.157
  44.0 0.1 fusion.156
  44.2 0.2 fusion.155
  44.3 0.1 fusion.154
  44.5 0.6 add_convert_fusion
  45.1 0.3 convolution_bitcast_fusion.19
  45.4 0.1 fusion.150
  45.5 0.0 copy-start.2
  45.6 0.6 copy-done.2
  46.2 0.2 convert_reduce_fusion
  46.4 0.2 fusion.14
  46.6 0.2 fusion.12
  46.8 0.2 fusion.10
  47.0 0.2 fusion.8
  47.2 0.2 fusion.6
  47.4 0.2 fusion.4
  47.6 0.0 collective-permute-done.2
  47.6 0.0 collective-permute-start.5
  47.7 0.0 collective-permute-done.3
  47.7 0.0 collective-permute-done.4
  47.8 4.8 %collective-permute-done.5 = bf16[8,16,2,128]{3,1,0,2:T(8,128)(2,1)S(1)} collective-permute-done((bf16[8,16,2,128]{3,1,0,2:T(8,128)(2,1)S(1)}, bf16[8,16,2,128]{3,1,0,2:T(8,128)(2,1)S(1)}, u32[]{:S(2)}, u32[]{:S(2)}) %collective-permute-start.5) | collective-permute-done | bytes 65568 | tf_op jit(solution)/shard_map/ppermute | solution.py:23
  52.6 0.2 convolution_bitcast_fusion.7
  52.8 0.2 convolution_bitcast_fusion.5
  53.0 0.2 convolution_bitcast_fusion.3
  53.2 0.2 convolution_bitcast_fusion.1
  53.4 0.0 collective-permute-done
  53.5 0.0 collective-permute-done.1
  53.5 0.2 convolution_bitcast_fusion.11
  53.8 0.2 fusion.18
  54.0 0.2 convolution_bitcast_fusion.9
  54.2 0.2 fusion.22
  54.4 0.2 fusion.26
  54.6 0.2 fusion.30
  54.8 0.2 fusion.34
  55.0 0.0 copy-start.1
  55.0 0.2 fusion.38
  55.2 0.6 copy-done.1
  55.8 0.8 convolution_convert_fusion.1
  56.7 0.3 convolution_convert_fusion
  56.9 0.1 copy.64
  57.1 29.2 %all_to_all.5 = bf16[8,2,128,128]{3,2,1,0:T(8,128)(2,1)S(1)} all-to-all(bf16[8,2,128,128]{3,2,1,0:T(8,128)(2,1)S(1)} %copy.64), channel_id=1, replica_groups=mesh['gx'=8,'gy'=16,'gz'=8] {'gx'}, dimensions={0} | all-to-all | bytes 1048576 | tf_op jit(solution)/shard_map/all_to_all | solution.py:121
  86.3 0.8 copy.115
  (19 shorter events, 0.2 us)
Async XLA Ops:
  0.0 19.0 %copy-start = (bf16[8,16,16,128]{3,2,1,0:T(8,128)(2,1)S(1)}, bf16[8,16,16,128]{3,2,1,0:T(8,128)(2,1)}, u32[]{:S(2)}) copy-start(bf16[8,16,16,128]{3,2,1,0:T(8,128)(2,1)} %param.3) | copy-start | bytes 1572868
  1.0 52.4 %collective-permute-start = (bf16[2,16,16,128]{3,2,1,0:T(8,128)(2,1)S(1)}, bf16[2,16,16,128]{3,2,1,0:T(8,128)(2,1)S(1)}, u32[]{:S(2)}, u32[]{:S(2)}) collective-permute-start(bf16[2,16,16,128]{3,2,1,0:T(8,128)(2,1)S(1)} %get-tuple-element.12), channel_id=1, source_target_pairs={{0,128},{128,256},{256,384},{384,512},{512,640},{640,768},{768,896... | collective-permute-start | bytes 393224 | tf_op jit(solution)/shard_map/ppermute | solution.py:22
  5.1 48.4 %collective-permute-start.1 = (bf16[2,16,16,128]{3,2,1,0:T(8,128)(2,1)S(1)}, bf16[2,16,16,128]{3,2,1,0:T(8,128)(2,1)S(1)}, u32[]{:S(2)}, u32[]{:S(2)}) collective-permute-start(bf16[2,16,16,128]{3,2,1,0:T(8,128)(2,1)S(1)} %get-tuple-element.11), channel_id=1, source_target_pairs={{128,0},{256,128},{384,256},{512,384},{640,512},{768,640},{896,768... | collective-permute-start | bytes 393224 | tf_op jit(solution)/shard_map/ppermute | solution.py:23
  19.1 28.5 %collective-permute-start.2 = (bf16[8,2,16,128]{3,2,0,1:T(8,128)(2,1)S(1)}, bf16[8,2,16,128]{3,2,0,1:T(8,128)(2,1)S(1)}, u32[]{:S(2)}, u32[]{:S(2)}) collective-permute-start(bf16[8,2,16,128]{3,2,0,1:T(8,128)(2,1)S(1)} %copy.86), channel_id=1, source_target_pairs={{0,8},{8,16},{16,24},{24,32},{32,40},{40,48},{48,56},{56,64},{64,7... | collective-permute-start | bytes 196616 | tf_op jit(solution)/shard_map/ppermute | solution.py:22
  32.1 15.6 %collective-permute-start.3 = (bf16[8,2,16,128]{3,2,0,1:T(8,128)(2,1)S(1)}, bf16[8,2,16,128]{3,2,0,1:T(8,128)(2,1)S(1)}, u32[]{:S(2)}, u32[]{:S(2)}) collective-permute-start(bf16[8,2,16,128]{3,2,0,1:T(8,128)(2,1)S(1)} %copy.87), channel_id=1, source_target_pairs={{8,0},{16,8},{24,16},{32,24},{40,32},{48,40},{56,48},{64,56},{72,6... | collective-permute-start | bytes 196616 | tf_op jit(solution)/shard_map/ppermute | solution.py:23
  37.1 10.7 %collective-permute-start.4 = (bf16[8,16,2,128]{3,1,0,2:T(8,128)(2,1)S(1)}, bf16[8,16,2,128]{3,1,0,2:T(8,128)(2,1)S(1)}, u32[]{:S(2)}, u32[]{:S(2)}) collective-permute-start(bf16[8,16,2,128]{3,1,0,2:T(8,128)(2,1)S(1)} %copy.88), channel_id=1, source_target_pairs={{0,1},{1,2},{2,3},{3,4},{4,5},{5,6},{6,7},{7,0},{8,9},{9,10},{10,1... | collective-permute-start | bytes 196616 | tf_op jit(solution)/shard_map/ppermute | solution.py:22
  45.5 0.7 copy-start.2
  47.6 4.9 %collective-permute-start.5 = (bf16[8,16,2,128]{3,1,0,2:T(8,128)(2,1)S(1)}, bf16[8,16,2,128]{3,1,0,2:T(8,128)(2,1)S(1)}, u32[]{:S(2)}, u32[]{:S(2)}) collective-permute-start(bf16[8,16,2,128]{3,1,0,2:T(8,128)(2,1)S(1)} %copy.89), channel_id=1, source_target_pairs={{1,0},{2,1},{3,2},{4,3},{5,4},{6,5},{7,6},{0,7},{9,8},{10,9},{11,1... | collective-permute-start | bytes 196616 | tf_op jit(solution)/shard_map/ppermute | solution.py:23
  55.0 0.8 copy-start.1
where the time goes:
time: 87.4 us; the launch traced here: 87.1 us
  starting transfers between devices  42.5 us (49%)
  blocking collectives  29.2 us (33%)
  matrix products  5.07 us (6%)
  waiting for transfers between devices  4.76 us (5%)
  local copies, waits for them, and re-layouts  4.3 us (5%)
    all_to_all x1, blocking collectives, local(): lax.all_to_all(chosen, 'gx', split_axis=0, concat_axis=0, tiled=True)  29.2 us
    ppermute x3, starting transfers between devices, with_halo(): lax.ppermute(last, axis, up)  23.7 us
    ppermute x3, starting transfers between devices, with_halo(): lax.ppermute(first, axis, [(b, a) for a, b in up])  18.8 us
    ppermute x3, waiting for transfers between devices, with_halo(): lax.ppermute(first, axis, [(b, a) for a, b in up])  4.76 us
    dot_general x19, matrix products, gram(): jnp.dot(left.reshape(-1, width).T, right.reshape(-1, right.shape[-1]), pr...  3.98 us
    unnamed x11, local copies, waits for them, and re-layouts  2.12 us
  transfers between devices with their start and end apart: 6, of which 1 were waited for; matrix products, arithmetic and copies ran while one was open for 5% of the time, Pallas kernels for 0%

commit v1 on v0

v1 whole, which is shorter than its diff:
```python
import functools
import math

import jax
import jax.numpy as jnp
from jax import lax
from jax.experimental import pallas as pl
from jax.experimental.pallas import tpu as pltpu
from jax.sharding import PartitionSpec as P

CAP = 2
SMOOTH = 0.25
MESH = pl.DeviceIdType.MESH
F32 = jnp.float32
BF16 = jnp.bfloat16


def dot(a, b):
    return jnp.dot(a, b, preferred_element_type=F32)


def gram(a, b):
    return lax.dot_general(a, b, (((0,), (0,)), ((), ())), preferred_element_type=F32)


def kernel(
    sizes,
    c_hbm,
    pot_hbm,
    own_hbm,
    out,
    c_v,
    s_v,
    pot_v,
    own_s,
    sel_s,
    x_rx,
    y_rx,
    z_tx,
    z_own,
    z_rx,
    ret_tx,
    ret_rx,
    prod,
    slots,
    load_sem,
    tx_sem,
    rx_sem,
    a2a_tx,
    a2a_rx,
):
    n_x, n_y, n_z = sizes
    cx, cy, cz, orb = c_hbm.shape
    p, q, r = (lax.axis_index(a) for a in ("gx", "gy", "gz"))
    low = q % 2 == 0
    x_lo, x_hi = ((p + n_x - 1) % n_x, q, r), ((p + 1) % n_x, q, r)
    y_lo, y_hi = (p, (q + n_y - 1) % n_y, r), (p, (q + 1) % n_y, r)
    z_lo, z_hi = (p, q, (r + n_z - 1) % n_z), (p, q, (r + 1) % n_z)

    loads = [
        pltpu.make_async_copy(c_hbm, c_v, load_sem.at[0]),
        pltpu.make_async_copy(pot_hbm, pot_v, load_sem.at[1]),
        pltpu.make_async_copy(own_hbm, own_s, load_sem.at[2]),
    ]
    for load in loads:
        load.start()

    barrier = pltpu.get_barrier_semaphore()
    for k in range(1, n_x):
        pl.semaphore_signal(barrier, inc=1, device_id=((p + k) % n_x, q, r), device_id_type=MESH)
    for peer in (z_lo, z_hi):
        pl.semaphore_signal(barrier, inc=1, device_id=peer, device_id_type=MESH)

    @pl.when(low)
    def _():
        for peer in (y_lo, y_hi):
            pl.semaphore_signal(barrier, inc=1, device_id=peer, device_id_type=MESH)

    def send(src, dst, sem, peer):
        return pltpu.make_async_remote_copy(
            src_ref=src,
            dst_ref=dst,
            send_sem=tx_sem.at[sem],
            recv_sem=rx_sem.at[sem],
            device_id=peer,
            device_id_type=MESH,
        )

    push_x = send(c_v.at[pl.ds(cx - 2, 2)], x_rx, 0, x_hi)
    push_z = [send(z_tx.at[0], z_rx.at[1], 1, z_lo), send(z_tx.at[1], z_rx.at[0], 2, z_hi)]
    back_x = send(ret_tx.at[0], ret_rx.at[0], 3, x_lo)
    push_y = [
        send(c_v.at[:, pl.ds(0, 2)], y_rx.at[1], 4, y_lo),
        send(c_v.at[:, pl.ds(cy - 2, 2)], y_rx.at[0], 5, y_hi),
    ]
    back_y = [
        send(ret_tx.at[1], ret_rx.at[2], 6, y_lo),
        send(ret_tx.at[2], ret_rx.at[1], 7, y_hi),
    ]

    loads[0].wait()
    pl.semaphore_wait(barrier, jnp.where(low, n_x + 1, n_x + 3))

    @pl.when(jnp.logical_not(low))
    def _():
        for copy in push_y:
            copy.start()

    push_x.start()

    layer = cy * cz
    row = lax.broadcasted_iota(jnp.int32, (layer, layer), 0)
    col = lax.broadcasted_iota(jnp.int32, (layer, layer), 1)
    apart = jnp.abs(row - col)
    beside = ((apart == 1) & (row // cz == col // cz)) | (apart == cz)
    stencil = jnp.where(apart == 0, 1.0, jnp.where(beside, SMOOTH, 0.0)).astype(BF16)
    face = cx * cz
    small = stencil[:face, :face]

    pr = lax.broadcasted_iota(jnp.int32, (4 * cy, layer), 0)
    pc = lax.broadcasted_iota(jnp.int32, (4 * cy, layer), 1)
    which = pr // cy
    wanted = jnp.where(which < 2, which, cz + 1 - which)
    pick = (pc == (pr % cy) * cz + wanted).astype(BF16)
    for x in range(cx):
        rows = dot(pick, c_v[x].reshape(layer, orb)).astype(BF16)
        at = pl.ds(x * cy, cy)
        for side in range(2):
            for k in range(2):
                m = (2 * side + k) * cy
                z_tx[side, k, at] = rows[m : m + cy]
    for copy in push_z:
        copy.start()

    loads[1].wait()
    loads[2].wait()

    blocks = own_s.shape[0]
    owners = [own_s[b] for b in range(blocks)]
    ranks = []
    for b in range(blocks):
        rank = jnp.int32(0)
        for e in range(b):
            rank = rank + (owners[e] == owners[b]).astype(jnp.int32)
        ranks.append(rank)
    for o in range(n_x):
        for k in range(CAP):
            index = jnp.int32(blocks)
            for b in range(blocks):
                index = jnp.where((owners[b] == o) & (ranks[b] == k), b, index)
            sel_s[o * CAP + k] = index
    prod[blocks] = jnp.zeros((orb, orb), BF16)

    lane = lax.broadcasted_iota(jnp.int32, (layer, cz), 1)
    cell = lax.broadcasted_iota(jnp.int32, (layer, cz), 0) % cz
    both = jnp.zeros((orb, 2 * orb), F32)
    for x in range(cx):
        beyond = jnp.zeros((layer, orb), F32)
        for n in (x - 1, x + 1):
            if 0 <= n < cx:
                beyond = beyond + c_v[n].reshape(layer, orb).astype(F32)
        smooth = (dot(stencil, c_v[x].reshape(layer, orb)) + SMOOTH * beyond).astype(BF16)
        s_v[x] = smooth.reshape(cy, cz, orb)
        spread = jnp.broadcast_to(pot_v[x][:, None, :], (cy, cz, cz)).reshape(layer, cz)
        value = jnp.sum(jnp.where(lane == cell, spread, 0.0), axis=1, keepdims=True)
        weighted = (value * smooth.astype(F32)).astype(BF16)
        both = both + gram(smooth, jnp.concatenate([smooth, weighted], axis=1))
        edge = dot(pick, smooth).astype(BF16)
        at = pl.ds(x * cy, cy)
        z_own[0, at] = edge[:cy]
        z_own[1, at] = edge[2 * cy : 3 * cy]
    hamilton = both[:, orb:].astype(BF16)

    c_edge = [
        c_v[0].reshape(layer, orb),
        c_v[cx - 1].reshape(layer, orb),
        c_v[:, 0].reshape(face, orb),
        c_v[:, cy - 1].reshape(face, orb),
        z_tx[0, 0],
        z_tx[1, 0],
    ]
    s_edge = [
        s_v[0].reshape(layer, orb),
        s_v[cx - 1].reshape(layer, orb),
        s_v[:, 0].reshape(face, orb),
        s_v[:, cy - 1].reshape(face, orb),
        z_own[0],
        z_own[1],
    ]
    edges = jnp.zeros((orb, orb), F32)
    for c in c_edge:
        edges = edges + gram(c, c)
    correlation = both[:, :orb] + SMOOTH * SMOOTH * edges
    diagonal = lax.broadcasted_iota(jnp.int32, (orb, orb), 0) == lax.broadcasted_iota(
        jnp.int32, (orb, orb), 1
    )
    scale = math.sqrt(cx * cy * cz)
    unit = jnp.where(diagonal, 1.0, 0.0)
    prod[0] = dot((scale * (correlation - unit)).astype(BF16), hamilton).astype(BF16)

    def multiply(block, deviation):
        prod[block] = dot(deviation, hamilton).astype(BF16)

    def meet(at, c_far, c_deep, matrix):
        s_far = (dot(matrix, c_far) + SMOOTH * c_deep.astype(F32)).astype(BF16)
        mine = jnp.concatenate([s_edge[at], c_edge[at]], axis=0)
        other = jnp.concatenate([c_far, s_far], axis=0)
        factor = scale * SMOOTH
        return (factor * gram(mine, other)).astype(BF16), mine, other, factor

    def turned(mine, other, factor):
        return (factor * gram(other, mine)).astype(BF16)

    push_x.wait_recv()
    deviation, *rest = meet(0, x_rx[1].reshape(layer, orb), x_rx[0].reshape(layer, orb), stencil)
    ret_tx[0] = turned(*rest)
    back_x.start()
    multiply(1, deviation)

    for side in range(2):
        push_z[1 - side].wait_recv()
        deviation, *_ = meet(4 + side, z_rx[side, 0], z_rx[side, 1], small)
        multiply(5 + side, deviation)

    back_x.wait_recv()
    multiply(2, ret_rx[0])

    @pl.when(low)
    def _():
        for side in range(2):
            push_y[1 - side].wait_recv()
            far, deep = (1, 0) if side == 0 else (0, 1)
            deviation, *rest = meet(
                2 + side,
                y_rx[side, :, far].reshape(face, orb),
                y_rx[side, :, deep].reshape(face, orb),
                small,
            )
            ret_tx[1 + side] = turned(*rest)
            back_y[side].start()
            multiply(3 + side, deviation)

    @pl.when(jnp.logical_not(low))
    def _():
        for side in range(2):
            back_y[1 - side].wait_recv()
            multiply(3 + side, ret_rx[1 + side])

    def hand(o):
        return pltpu.make_async_remote_copy(
            src_ref=slots.at[o],
            dst_ref=out.at[pl.ds(CAP * p, CAP)],
            send_sem=a2a_tx.at[o],
            recv_sem=a2a_rx.at[p],
            device_id=(o, q, r),
            device_id_type=MESH,
        )

    for o in range(n_x):

        @pl.when(o != p)
        def _():
            for k in range(CAP):
                slots[o, k] = prod[sel_s[o * CAP + k]]
            hand(o).start()

    for k in range(CAP):
        out[CAP * p + k] = prod[sel_s[CAP * p + k]]

    push_x.wait_send()
    back_x.wait_send()
    for copy in push_z:
        copy.wait_send()

    @pl.when(low)
    def _():
        for copy in back_y:
            copy.wait_send()

    @pl.when(jnp.logical_not(low))
    def _():
        for copy in push_y:
            copy.wait_send()

    for o in range(n_x):

        @pl.when(o != p)
        def _():
            hand(o).wait_send()
            pltpu.make_async_remote_copy(
                src_ref=slots.at[o],
                dst_ref=out.at[pl.ds(CAP * o, CAP)],
                send_sem=a2a_tx.at[o],
                recv_sem=a2a_rx.at[o],
                device_id=(o, q, r),
                device_id_type=MESH,
            ).wait_recv()


def local(coefficients, potential, owner_map):
    sizes = tuple(lax.axis_size(a) for a in ("gx", "gy", "gz"))
    cx, cy, cz, orb = coefficients.shape
    blocks = owner_map.size
    n_x = sizes[0]
    result = pl.pallas_call(
        functools.partial(kernel, sizes),
        out_shape=jax.ShapeDtypeStruct((n_x * CAP, orb, orb), BF16),
        in_specs=[pl.BlockSpec(memory_space=pl.ANY)] * 3,
        out_specs=pl.BlockSpec(memory_space=pltpu.VMEM),
        scratch_shapes=[
            pltpu.VMEM((cx, cy, cz, orb), BF16),
            pltpu.VMEM((cx, cy, cz, orb), BF16),
            pltpu.VMEM((cx, cy, cz), F32),
            pltpu.SMEM((blocks,), jnp.int32),
            pltpu.SMEM((n_x * CAP,), jnp.int32),
            pltpu.VMEM((2, cy, cz, orb), BF16),
            pltpu.VMEM((2, cx, 2, cz, orb), BF16),
            pltpu.VMEM((2, 2, cx * cy, orb), BF16),
            pltpu.VMEM((2, cx * cy, orb), BF16),
            pltpu.VMEM((2, 2, cx * cy, orb), BF16),
            pltpu.VMEM((3, orb, orb), BF16),
            pltpu.VMEM((3, orb, orb), BF16),
            pltpu.VMEM((blocks + 1, orb, orb), BF16),
            pltpu.VMEM((n_x, CAP, orb, orb), BF16),
            pltpu.SemaphoreType.DMA((3,)),
            pltpu.SemaphoreType.DMA((8,)),
            pltpu.SemaphoreType.DMA((8,)),
            pltpu.SemaphoreType.DMA((n_x,)),
            pltpu.SemaphoreType.DMA((n_x,)),
        ],
        compiler_params=pltpu.CompilerParams(
            collective_id=0, has_side_effects=True
        ),
        name="correction",
    )(coefficients, potential, owner_map.reshape(blocks))
    return result.reshape(1, 1, 1, n_x * CAP, orb, orb)


def solution(mesh):
    in_specs = (P("gx", "gy", "gz", None), P("gx", "gy", "gz"), P("gx", "gy", "gz", None, None))
    out_specs = P("gx", "gy", "gz", None, None, None)
    return jax.shard_map(local, mesh=mesh, in_specs=in_specs, out_specs=out_specs, check_vma=False)
```

time: 87.4 us -> 63.2 us (0.72)
  the two profiles are of different devices: /device:TPU:7 before, /device:TPU:65 now
where the time goes in v1:
time: 63.2 us; the launch traced here: 63 us
  Pallas kernels  61.1 us (97%)
  local copies, waits for them, and re-layouts  1.89 us (3%)
    pallas_call x1, Pallas kernels, local(): pl.pallas_call(functools.partial(kernel, sizes), out_shape=jax.ShapeDtype...  61.1 us
    unnamed x1, local copies, waits for them, and re-layouts  1.89 us

profile of v1, /device:TPU:65, one launch (start us, length us, event | category | flops | bytes accessed | tf_op | source)
XLA Modules:
  0.0 63.0 jit_solution(4349938110481668331)
XLA Ops:
  0.0 61.1 %correction.1 = bf16[16,128,128]{2,1,0:T(8,128)(2,1)} custom-call(bf16[8,16,16,128]{3,2,1,0:T(8,128)(2,1)} %c_hbm.1, f32[8,16,16]{2,1,0:T(8,128)} %pot_hbm.1, s32[7]{0:T(128)} %bitcast.3), custom_call_target="tpu_custom_call" | custom-call | tf_op jit(solution)/shard_map/correction/pallas_call | solution.py:305
  61.1 1.9 %copy.5 = bf16[1,1,1,16,128,128]{5,4,3,2,1,0:T(8,128)(2,1)} copy(bf16[1,1,1,16,128,128]{5,4,3,2,1,0:T(8,128)(2,1)} %bitcast.2) | data formatting | bytes 1048576

commit v2 on v1

--- a/solution.py
+++ b/solution.py
@@ -48,6 +48,7 @@
     rx_sem,
     a2a_tx,
     a2a_rx,
+    ready,
 ):
     n_x, n_y, n_z = sizes
     cx, cy, cz, orb = c_hbm.shape
@@ -65,11 +66,24 @@
     for load in loads:
         load.start()
 
+    def made_above(pair):
+        return pair < n_x // 2
+
+    up_lo, up_hi = made_above((p + n_x - 1) % n_x), made_above(p)
+
     barrier = pltpu.get_barrier_semaphore()
-    for k in range(1, n_x):
-        pl.semaphore_signal(barrier, inc=1, device_id=((p + k) % n_x, q, r), device_id_type=MESH)
-    for peer in (z_lo, z_hi):
-        pl.semaphore_signal(barrier, inc=1, device_id=peer, device_id_type=MESH)
+    for o in range(1, n_x):
+
+        @pl.when(o > p)
+        def _():
+            pl.semaphore_signal(barrier, inc=1, device_id=(o, q, r), device_id_type=MESH)
+
+    pl.semaphore_signal(barrier, inc=1, device_id=z_hi, device_id_type=MESH)
+    behind = jnp.logical_not(low) & (r % 2 == 1)
+
+    @pl.when(jnp.logical_not(behind))
+    def _():
+        pl.semaphore_signal(barrier, inc=1, device_id=z_lo, device_id_type=MESH)
 
     @pl.when(low)
     def _():
@@ -86,27 +100,44 @@
             device_id_type=MESH,
         )
 
-    push_x = send(c_v.at[pl.ds(cx - 2, 2)], x_rx, 0, x_hi)
+    push_x_hi = send(c_v.at[pl.ds(cx - 2, 2)], x_rx.at[0], 0, x_hi)
+    push_x_lo = send(c_v.at[pl.ds(0, 2)], x_rx.at[1], 3, x_lo)
     push_z = [send(z_tx.at[0], z_rx.at[1], 1, z_lo), send(z_tx.at[1], z_rx.at[0], 2, z_hi)]
-    back_x = send(ret_tx.at[0], ret_rx.at[0], 3, x_lo)
+    back_x_lo = send(ret_tx.at[0], ret_rx.at[1], 8, x_lo)
+    back_x_hi = send(ret_tx.at[1], ret_rx.at[0], 9, x_hi)
     push_y = [
         send(c_v.at[:, pl.ds(0, 2)], y_rx.at[1], 4, y_lo),
         send(c_v.at[:, pl.ds(cy - 2, 2)], y_rx.at[0], 5, y_hi),
     ]
     back_y = [
-        send(ret_tx.at[1], ret_rx.at[2], 6, y_lo),
-        send(ret_tx.at[2], ret_rx.at[1], 7, y_hi),
+        send(ret_tx.at[2], ret_rx.at[3], 6, y_lo),
+        send(ret_tx.at[3], ret_rx.at[2], 7, y_hi),
     ]
 
     loads[0].wait()
-    pl.semaphore_wait(barrier, jnp.where(low, n_x + 1, n_x + 3))
+    pl.semaphore_wait(barrier, p + jnp.where(low, 2, 4))
 
     @pl.when(jnp.logical_not(low))
     def _():
         for copy in push_y:
             copy.start()
 
-    push_x.start()
+    @pl.when(behind)
+    def _():
+        for copy in push_y:
+            copy.wait_send()
+        pl.semaphore_signal(barrier, inc=1, device_id=z_lo, device_id_type=MESH)
+
+    @pl.when(jnp.logical_not(up_lo) & (p > 0))
+    def _():
+        push_x_lo.start()
+
+    for o in range(n_x - 1):
+
+        @pl.when(o < p)
+        def _():
+            which = jnp.where(o == p - 1, 0, jnp.where((o == 0) & (p == n_x - 1), 2, 1))
+            pl.semaphore_signal(ready.at[which], inc=1, device_id=(o, q, r), device_id_type=MESH)
 
     layer = cy * cz
     row = lax.broadcasted_iota(jnp.int32, (layer, layer), 0)
@@ -131,6 +162,14 @@
                 z_tx[side, k, at] = rows[m : m + cy]
     for copy in push_z:
         copy.start()
+
+    @pl.when(p < n_x - 1)
+    def _():
+        pl.semaphore_wait(ready.at[0], 1)
+
+    @pl.when(up_hi)
+    def _():
+        push_x_hi.start()
 
     loads[1].wait()
     loads[2].wait()
@@ -170,6 +209,11 @@
         z_own[0, at] = edge[:cy]
         z_own[1, at] = edge[2 * cy : 3 * cy]
     hamilton = both[:, orb:].astype(BF16)
+
+    @pl.when(p == 0)
+    def _():
+        pl.semaphore_wait(ready.at[2], 1)
+        push_x_lo.start()
 
     c_edge = [
         c_v[0].reshape(layer, orb),
@@ -211,19 +255,36 @@
     def turned(mine, other, factor):
         return (factor * gram(other, mine)).astype(BF16)
 
-    push_x.wait_recv()
-    deviation, *rest = meet(0, x_rx[1].reshape(layer, orb), x_rx[0].reshape(layer, orb), stencil)
-    ret_tx[0] = turned(*rest)
-    back_x.start()
-    multiply(1, deviation)
+    @pl.when(up_lo)
+    def _():
+        push_x_hi.wait_recv()
+        deviation, *rest = meet(0, x_rx[0, 1].reshape(layer, orb), x_rx[0, 0].reshape(layer, orb), stencil)
+        ret_tx[0] = turned(*rest)
+        back_x_lo.start()
+        multiply(1, deviation)
+
+    @pl.when(jnp.logical_not(up_hi))
+    def _():
+        push_x_lo.wait_recv()
+        deviation, *rest = meet(1, x_rx[1, 0].reshape(layer, orb), x_rx[1, 1].reshape(layer, orb), stencil)
+        ret_tx[1] = turned(*rest)
+        back_x_hi.start()
+        multiply(2, deviation)
 
     for side in range(2):
         push_z[1 - side].wait_recv()
         deviation, *_ = meet(4 + side, z_rx[side, 0], z_rx[side, 1], small)
         multiply(5 + side, deviation)
 
-    back_x.wait_recv()
-    multiply(2, ret_rx[0])
+    @pl.when(up_hi)
+    def _():
+        back_x_lo.wait_recv()
+        multiply(2, ret_rx[1])
+
+    @pl.when(jnp.logical_not(up_lo))
+    def _():
+        back_x_hi.wait_recv()
+        multiply(1, ret_rx[0])
 
     @pl.when(low)
     def _():
@@ -236,7 +297,7 @@
                 y_rx[side, :, deep].reshape(face, orb),
                 small,
             )
-            ret_tx[1 + side] = turned(*rest)
+            ret_tx[2 + side] = turned(*rest)
             back_y[side].start()
             multiply(3 + side, deviation)
 
@@ -244,7 +305,11 @@
     def _():
         for side in range(2):
             back_y[1 - side].wait_recv()
-            multiply(3 + side, ret_rx[1 + side])
+            multiply(3 + side, ret_rx[2 + side])
+
+    @pl.when(p < n_x - 2)
+    def _():
+        pl.semaphore_wait(ready.at[1], n_x - 2 - p - jnp.where(p == 0, 1, 0))
 
     def hand(o):
         return pltpu.make_async_remote_copy(
@@ -267,19 +332,33 @@
     for k in range(CAP):
         out[CAP * p + k] = prod[sel_s[CAP * p + k]]
 
-    push_x.wait_send()
-    back_x.wait_send()
     for copy in push_z:
         copy.wait_send()
 
+    @pl.when(up_hi)
+    def _():
+        push_x_hi.wait_send()
+
+    @pl.when(jnp.logical_not(up_hi))
+    def _():
+        back_x_hi.wait_send()
+
+    @pl.when(up_lo)
+    def _():
+        back_x_lo.wait_send()
+
+    @pl.when(jnp.logical_not(up_lo))
+    def _():
+        push_x_lo.wait_send()
+
+    @pl.when(jnp.logical_not(low) & jnp.logical_not(behind))
+    def _():
+        for copy in push_y:
+            copy.wait_send()
+
     @pl.when(low)
     def _():
         for copy in back_y:
-            copy.wait_send()
-
-    @pl.when(jnp.logical_not(low))
-    def _():
-        for copy in push_y:
             copy.wait_send()
 
     for o in range(n_x):
@@ -313,23 +392,24 @@
             pltpu.VMEM((cx, cy, cz), F32),
             pltpu.SMEM((blocks,), jnp.int32),
             pltpu.SMEM((n_x * CAP,), jnp.int32),
-            pltpu.VMEM((2, cy, cz, orb), BF16),
+            pltpu.VMEM((2, 2, cy, cz, orb), BF16),
             pltpu.VMEM((2, cx, 2, cz, orb), BF16),
             pltpu.VMEM((2, 2, cx * cy, orb), BF16),
             pltpu.VMEM((2, cx * cy, orb), BF16),
             pltpu.VMEM((2, 2, cx * cy, orb), BF16),
-            pltpu.VMEM((3, orb, orb), BF16),
-            pltpu.VMEM((3, orb, orb), BF16),
+            pltpu.VMEM((4, orb, orb), BF16),
+            pltpu.VMEM((4, orb, orb), BF16),
             pltpu.VMEM((blocks + 1, orb, orb), BF16),
             pltpu.VMEM((n_x, CAP, orb, orb), BF16),
             pltpu.SemaphoreType.DMA((3,)),
-            pltpu.SemaphoreType.DMA((8,)),
-            pltpu.SemaphoreType.DMA((8,)),
+            pltpu.SemaphoreType.DMA((10,)),
+            pltpu.SemaphoreType.DMA((10,)),
             pltpu.SemaphoreType.DMA((n_x,)),
             pltpu.SemaphoreType.DMA((n_x,)),
+            pltpu.SemaphoreType.REGULAR((3,)),
         ],
         compiler_params=pltpu.CompilerParams(
-            collective_id=0, has_side_effects=True
+            collective_id=0, has_side_effects=True, vmem_limit_bytes=53 * 1024 * 1024
         ),
         name="correction",
     )(coefficients, potential, owner_map.reshape(blocks))

time: 63.2 us -> 57.4 us (0.908)
  the two profiles are of different devices: /device:TPU:65 before, /device:TPU:66 now
where the time goes in v2:
time: 57.4 us; the launch traced here: 57.2 us
  Pallas kernels  54.9 us (96%)
  local copies, waits for them, and re-layouts  2.29 us (4%)
    pallas_call x1, Pallas kernels, local(): pl.pallas_call(functools.partial(kernel, sizes), out_shape=jax.ShapeDtype...  54.9 us
    unnamed x5, local copies, waits for them, and re-layouts  2.29 us

profile of v2, /device:TPU:66, one launch (start us, length us, event | category | flops | bytes accessed | tf_op | source)
XLA Modules:
  0.0 57.2 jit_solution(9284450020309036427)
XLA Ops:
  0.0 0.0 copy-start.1
  0.0 0.7 %copy-done.1 = s32[1,1,1,7,1]{3,4,2,1,0:T(1,128)S(1)} copy-done((s32[1,1,1,7,1]{3,4,2,1,0:T(1,128)S(1)}, s32[1,1,1,7,1]{3,4,2,1,0:T(1,128)}, u32[]{:S(2)}) %copy-start.1) | copy-done | bytes 52
  0.7 0.0 copy-start
  0.7 0.8 %copy-done = f32[8,16,16]{2,1,0:T(8,128)S(1)} copy-done((f32[8,16,16]{2,1,0:T(8,128)S(1)}, f32[8,16,16]{2,1,0:T(8,128)}, u32[]{:S(2)}) %copy-start) | copy-done | bytes 8216
  1.5 54.9 %correction.1 = bf16[16,128,128]{2,1,0:T(8,128)(2,1)S(1)} custom-call(bf16[8,16,16,128]{3,2,1,0:T(8,128)(2,1)} %c_hbm.1, f32[8,16,16]{2,1,0:T(8,128)S(1)} %copy-done, s32[7]{0:T(128)S(1)} %bitcast.3), custom_call_target="tpu_custom_call" | custom-call | tf_op jit(solution)/shard_map/correction/pallas_call | solution.py:384
  56.4 0.8 %copy.5 = bf16[1,1,1,16,128,128]{5,4,3,2,1,0:T(8,128)(2,1)} copy(bf16[1,1,1,16,128,128]{5,4,3,2,1,0:T(8,128)(2,1)S(1)} %bitcast.2) | data formatting | bytes 1048576
Async XLA Ops:
  0.0 0.7 %copy-start.1 = (s32[1,1,1,7,1]{3,4,2,1,0:T(1,128)S(1)}, s32[1,1,1,7,1]{3,4,2,1,0:T(1,128)}, u32[]{:S(2)}) copy-start(s32[1,1,1,7,1]{3,4,2,1,0:T(1,128)} %param.5) | copy-start | bytes 88
  0.7 0.8 %copy-start = (f32[8,16,16]{2,1,0:T(8,128)S(1)}, f32[8,16,16]{2,1,0:T(8,128)}, u32[]{:S(2)}) copy-start(f32[8,16,16]{2,1,0:T(8,128)} %pot_hbm.1) | copy-start | bytes 24580

commit v3 on v2

--- a/solution.py
+++ b/solution.py
@@ -49,6 +49,7 @@
     a2a_tx,
     a2a_rx,
     ready,
+    go,
 ):
     n_x, n_y, n_z = sizes
     cx, cy, cz, orb = c_hbm.shape
@@ -78,12 +79,17 @@
         def _():
             pl.semaphore_signal(barrier, inc=1, device_id=(o, q, r), device_id_type=MESH)
 
-    pl.semaphore_signal(barrier, inc=1, device_id=z_hi, device_id_type=MESH)
-    behind = jnp.logical_not(low) & (r % 2 == 1)
-
-    @pl.when(jnp.logical_not(behind))
-    def _():
-        pl.semaphore_signal(barrier, inc=1, device_id=z_lo, device_id_type=MESH)
+    for peer in (z_lo, z_hi):
+        pl.semaphore_signal(barrier, inc=1, device_id=peer, device_id_type=MESH)
+
+    even = p % 2 == 0
+    first = jnp.logical_not(low) & (r % 2 == 1)
+    second = jnp.logical_not(low) & (r % 2 == 0)
+    for o in range(2, n_x, 2):
+
+        @pl.when(second & even & (o > p))
+        def _():
+            pl.semaphore_signal(barrier, inc=1, device_id=(o, q, z_hi[2]), device_id_type=MESH)
 
     @pl.when(low)
     def _():
@@ -114,23 +120,7 @@
         send(ret_tx.at[3], ret_rx.at[2], 7, y_hi),
     ]
 
-    loads[0].wait()
-    pl.semaphore_wait(barrier, p + jnp.where(low, 2, 4))
-
-    @pl.when(jnp.logical_not(low))
-    def _():
-        for copy in push_y:
-            copy.start()
-
-    @pl.when(behind)
-    def _():
-        for copy in push_y:
-            copy.wait_send()
-        pl.semaphore_signal(barrier, inc=1, device_id=z_lo, device_id_type=MESH)
-
-    @pl.when(jnp.logical_not(up_lo) & (p > 0))
-    def _():
-        push_x_lo.start()
+    pl.semaphore_wait(barrier, p + jnp.where(low, 2, 4) + jnp.where(first & even, p // 2, 0))
 
     for o in range(n_x - 1):
 
@@ -138,6 +128,17 @@
         def _():
             which = jnp.where(o == p - 1, 0, jnp.where((o == 0) & (p == n_x - 1), 2, 1))
             pl.semaphore_signal(ready.at[which], inc=1, device_id=(o, q, r), device_id_type=MESH)
+
+    loads[0].wait()
+
+    @pl.when(first)
+    def _():
+        for copy in reversed(push_y):
+            copy.start()
+
+    @pl.when(jnp.logical_not(up_lo) & (p > 0))
+    def _():
+        push_x_lo.start()
 
     layer = cy * cz
     row = lax.broadcasted_iota(jnp.int32, (layer, layer), 0)
@@ -163,6 +164,16 @@
     for copy in push_z:
         copy.start()
 
+    @pl.when(first)
+    def _():
+        for copy in push_y:
+            copy.wait_send()
+        for o in range(n_x):
+
+            @pl.when((o == p) | (even & (o % 2 == 0) & (o < p)))
+            def _():
+                pl.semaphore_signal(go, inc=1, device_id=(o, q, z_lo[2]), device_id_type=MESH)
+
     @pl.when(p < n_x - 1)
     def _():
         pl.semaphore_wait(ready.at[0], 1)
@@ -170,6 +181,12 @@
     @pl.when(up_hi)
     def _():
         push_x_hi.start()
+
+    @pl.when(second)
+    def _():
+        pl.semaphore_wait(go, jnp.where(even, (n_x - p + 1) // 2, 1))
+        for copy in reversed(push_y):
+            copy.start()
 
     loads[1].wait()
     loads[2].wait()
@@ -351,7 +368,7 @@
     def _():
         push_x_lo.wait_send()
 
-    @pl.when(jnp.logical_not(low) & jnp.logical_not(behind))
+    @pl.when(second)
     def _():
         for copy in push_y:
             copy.wait_send()
@@ -407,6 +424,7 @@
             pltpu.SemaphoreType.DMA((n_x,)),
             pltpu.SemaphoreType.DMA((n_x,)),
             pltpu.SemaphoreType.REGULAR((3,)),
+            pltpu.SemaphoreType.REGULAR,
         ],
         compiler_params=pltpu.CompilerParams(
             collective_id=0, has_side_effects=True, vmem_limit_bytes=53 * 1024 * 1024

time: 57.4 us -> 56 us (0.976)
  the two profiles are of different devices: /device:TPU:66 before, /device:TPU:68 now
where the time goes in v3:
time: 56 us; the launch traced here: 55.7 us
  Pallas kernels  53.4 us (95%)
  local copies, waits for them, and re-layouts  2.29 us (4%)
    pallas_call x1, Pallas kernels, local(): pl.pallas_call(functools.partial(kernel, sizes), out_shape=jax.ShapeDtype...  53.4 us
    unnamed x5, local copies, waits for them, and re-layouts  2.29 us

profile of v3, /device:TPU:68, one launch (start us, length us, event | category | flops | bytes accessed | tf_op | source)
XLA Modules:
  0.0 55.7 jit_solution(72261453148740777)
XLA Ops:
  0.0 0.0 copy-start.1
  0.0 0.7 %copy-done.1 = s32[1,1,1,7,1]{3,4,2,1,0:T(1,128)S(1)} copy-done((s32[1,1,1,7,1]{3,4,2,1,0:T(1,128)S(1)}, s32[1,1,1,7,1]{3,4,2,1,0:T(1,128)}, u32[]{:S(2)}) %copy-start.1) | copy-done | bytes 52
  0.7 0.0 copy-start
  0.7 0.8 %copy-done = f32[8,16,16]{2,1,0:T(8,128)S(1)} copy-done((f32[8,16,16]{2,1,0:T(8,128)S(1)}, f32[8,16,16]{2,1,0:T(8,128)}, u32[]{:S(2)}) %copy-start) | copy-done | bytes 8216
  1.5 53.4 %correction.1 = bf16[16,128,128]{2,1,0:T(8,128)(2,1)S(1)} custom-call(bf16[8,16,16,128]{3,2,1,0:T(8,128)(2,1)} %c_hbm.1, f32[8,16,16]{2,1,0:T(8,128)S(1)} %copy-done, s32[7]{0:T(128)S(1)} %bitcast.3), custom_call_target="tpu_custom_call" | custom-call | tf_op jit(solution)/shard_map/correction/pallas_call | solution.py:401
  54.9 0.8 %copy.5 = bf16[1,1,1,16,128,128]{5,4,3,2,1,0:T(8,128)(2,1)} copy(bf16[1,1,1,16,128,128]{5,4,3,2,1,0:T(8,128)(2,1)S(1)} %bitcast.2) | data formatting | bytes 1048576
Async XLA Ops:
  0.0 0.7 %copy-start.1 = (s32[1,1,1,7,1]{3,4,2,1,0:T(1,128)S(1)}, s32[1,1,1,7,1]{3,4,2,1,0:T(1,128)}, u32[]{:S(2)}) copy-start(s32[1,1,1,7,1]{3,4,2,1,0:T(1,128)} %param.5) | copy-start | bytes 88
  0.7 0.8 %copy-start = (f32[8,16,16]{2,1,0:T(8,128)S(1)}, f32[8,16,16]{2,1,0:T(8,128)}, u32[]{:S(2)}) copy-start(f32[8,16,16]{2,1,0:T(8,128)} %pot_hbm.1) | copy-start | bytes 24580

commit v4 on v3

--- a/solution.py
+++ b/solution.py
@@ -50,6 +50,10 @@
     a2a_rx,
     ready,
     go,
+    relayed,
+    relay_ok,
+    relay_tx,
+    relay_rx,
 ):
     n_x, n_y, n_z = sizes
     cx, cy, cz, orb = c_hbm.shape
@@ -120,7 +124,22 @@
         send(ret_tx.at[3], ret_rx.at[2], 7, y_hi),
     ]
 
-    pl.semaphore_wait(barrier, p + jnp.where(low, 2, 4) + jnp.where(first & even, p // 2, 0))
+    last, middle = n_x - 1, n_x // 2
+    routed = low & (p == last)
+    relay = jnp.logical_not(low) & (p == middle)
+
+    @pl.when(low & ((p < 2) | (p == last)))
+    def _():
+        peer = (middle, y_hi[1], r)
+        pl.semaphore_signal(barrier, inc=1, device_id=peer, device_id_type=MESH)
+
+    known = p + jnp.where(low, 2, 4) + jnp.where(first & even, p // 2, 0)
+    pl.semaphore_wait(barrier, known + jnp.where(relay, 3, 0))
+
+    @pl.when(relay)
+    def _():
+        peer = (last, y_lo[1], r)
+        pl.semaphore_signal(relay_ok, inc=1, device_id=peer, device_id_type=MESH)
 
     for o in range(n_x - 1):
 
@@ -170,7 +189,7 @@
             copy.wait_send()
         for o in range(n_x):
 
-            @pl.when((o == p) | (even & (o % 2 == 0) & (o < p)))
+            @pl.when((o == p) | (even & (o % 2 == 0) & (o < p) & (p < n_x - 2)))
             def _():
                 pl.semaphore_signal(go, inc=1, device_id=(o, q, z_lo[2]), device_id_type=MESH)
 
@@ -184,7 +203,7 @@
 
     @pl.when(second)
     def _():
-        pl.semaphore_wait(go, jnp.where(even, (n_x - p + 1) // 2, 1))
+        pl.semaphore_wait(go, jnp.where(even & (p < n_x - 2), (n_x - 1 - p) // 2, 1))
         for copy in reversed(push_y):
             copy.start()
 
@@ -318,6 +337,32 @@
             back_y[side].start()
             multiply(3 + side, deviation)
 
+    def to_relay(o):
+        return pltpu.make_async_remote_copy(
+            src_ref=slots.at[o],
+            dst_ref=relayed.at[o],
+            send_sem=a2a_tx.at[o],
+            recv_sem=relay_rx.at[o],
+            device_id=(middle, y_hi[1], r),
+            device_id_type=MESH,
+        )
+
+    def from_relay(o):
+        return pltpu.make_async_remote_copy(
+            src_ref=relayed.at[o],
+            dst_ref=out.at[pl.ds(CAP * last, CAP)],
+            send_sem=relay_tx.at[o],
+            recv_sem=a2a_rx.at[last],
+            device_id=(o, y_lo[1], r),
+            device_id_type=MESH,
+        )
+
+    @pl.when(relay)
+    def _():
+        for o in range(2):
+            to_relay(o).wait_recv()
+            from_relay(o).start()
+
     @pl.when(jnp.logical_not(low))
     def _():
         for side in range(2):
@@ -338,9 +383,17 @@
             device_id_type=MESH,
         )
 
+    @pl.when(routed)
+    def _():
+        pl.semaphore_wait(relay_ok, 1)
+        for o in range(2):
+            for k in range(CAP):
+                slots[o, k] = prod[sel_s[o * CAP + k]]
+            to_relay(o).start()
+
     for o in range(n_x):
 
-        @pl.when(o != p)
+        @pl.when((o != p) & jnp.logical_not(routed & (o < 2)))
         def _():
             for k in range(CAP):
                 slots[o, k] = prod[sel_s[o * CAP + k]]
@@ -351,6 +404,11 @@
 
     for copy in push_z:
         copy.wait_send()
+
+    @pl.when(relay)
+    def _():
+        for o in range(2):
+            from_relay(o).wait_send()
 
     @pl.when(up_hi)
     def _():
@@ -425,6 +483,10 @@
             pltpu.SemaphoreType.DMA((n_x,)),
             pltpu.SemaphoreType.REGULAR((3,)),
             pltpu.SemaphoreType.REGULAR,
+            pltpu.VMEM((2, CAP, orb, orb), BF16),
+            pltpu.SemaphoreType.REGULAR,
+            pltpu.SemaphoreType.DMA((2,)),
+            pltpu.SemaphoreType.DMA((2,)),
         ],
         compiler_params=pltpu.CompilerParams(
             collective_id=0, has_side_effects=True, vmem_limit_bytes=53 * 1024 * 1024

time: 56 us -> 54.4 us (0.971)
  the two profiles are of different devices: /device:TPU:68 before, /device:TPU:192 now
where the time goes in v4:
time: 54.4 us; the launch traced here: 54.1 us
  Pallas kernels  51.8 us (95%)
  local copies, waits for them, and re-layouts  2.29 us (4%)
    pallas_call x1, Pallas kernels, local(): pl.pallas_call(functools.partial(kernel, sizes), out_shape=jax.ShapeDtype...  51.8 us
    unnamed x5, local copies, waits for them, and re-layouts  2.29 us

profile of v4, /device:TPU:192, one launch (start us, length us, event | category | flops | bytes accessed | tf_op | source)
XLA Modules:
  0.0 54.1 jit_solution(6158430660448426689)
XLA Ops:
  0.0 0.0 copy-start.1
  0.0 0.7 %copy-done.1 = s32[1,1,1,7,1]{3,4,2,1,0:T(1,128)S(1)} copy-done((s32[1,1,1,7,1]{3,4,2,1,0:T(1,128)S(1)}, s32[1,1,1,7,1]{3,4,2,1,0:T(1,128)}, u32[]{:S(2)}) %copy-start.1) | copy-done | bytes 52
  0.7 0.0 copy-start
  0.7 0.8 %copy-done = f32[8,16,16]{2,1,0:T(8,128)S(1)} copy-done((f32[8,16,16]{2,1,0:T(8,128)S(1)}, f32[8,16,16]{2,1,0:T(8,128)}, u32[]{:S(2)}) %copy-start) | copy-done | bytes 8216
  1.5 51.8 %correction.1 = bf16[16,128,128]{2,1,0:T(8,128)(2,1)S(1)} custom-call(bf16[8,16,16,128]{3,2,1,0:T(8,128)(2,1)} %c_hbm.1, f32[8,16,16]{2,1,0:T(8,128)S(1)} %copy-done, s32[7]{0:T(128)S(1)} %bitcast.3), custom_call_target="tpu_custom_call" | custom-call | tf_op jit(solution)/shard_map/correction/pallas_call | solution.py:459
  53.3 0.8 %copy.5 = bf16[1,1,1,16,128,128]{5,4,3,2,1,0:T(8,128)(2,1)} copy(bf16[1,1,1,16,128,128]{5,4,3,2,1,0:T(8,128)(2,1)S(1)} %bitcast.2) | data formatting | bytes 1048576
Async XLA Ops:
  0.0 0.7 %copy-start.1 = (s32[1,1,1,7,1]{3,4,2,1,0:T(1,128)S(1)}, s32[1,1,1,7,1]{3,4,2,1,0:T(1,128)}, u32[]{:S(2)}) copy-start(s32[1,1,1,7,1]{3,4,2,1,0:T(1,128)} %param.5) | copy-start | bytes 88
  0.7 0.8 %copy-start = (f32[8,16,16]{2,1,0:T(8,128)S(1)}, f32[8,16,16]{2,1,0:T(8,128)}, u32[]{:S(2)}) copy-start(f32[8,16,16]{2,1,0:T(8,128)} %pot_hbm.1) | copy-start | bytes 24580

commit v5 on v4

--- a/solution.py
+++ b/solution.py
@@ -83,8 +83,12 @@
         def _():
             pl.semaphore_signal(barrier, inc=1, device_id=(o, q, r), device_id_type=MESH)
 
-    for peer in (z_lo, z_hi):
-        pl.semaphore_signal(barrier, inc=1, device_id=peer, device_id_type=MESH)
+    beside_z = ((z_lo, r == 0), (z_hi, r < n_z - 1))
+    for peer, higher in beside_z:
+
+        @pl.when(low | higher)
+        def _():
+            pl.semaphore_signal(barrier, inc=1, device_id=peer, device_id_type=MESH)
 
     even = p % 2 == 0
     first = jnp.logical_not(low) & (r % 2 == 1)
@@ -133,7 +137,8 @@
         peer = (middle, y_hi[1], r)
         pl.semaphore_signal(barrier, inc=1, device_id=peer, device_id_type=MESH)
 
-    known = p + jnp.where(low, 2, 4) + jnp.where(first & even, p // 2, 0)
+    lower_z = jnp.where(r == 0, 0, jnp.where(r == n_z - 1, 2, 1))
+    known = p + 2 + jnp.where(low, 0, lower_z) + jnp.where(first & even, p // 2, 0)
     pl.semaphore_wait(barrier, known + jnp.where(relay, 3, 0))
 
     @pl.when(relay)
@@ -147,6 +152,12 @@
         def _():
             which = jnp.where(o == p - 1, 0, jnp.where((o == 0) & (p == n_x - 1), 2, 1))
             pl.semaphore_signal(ready.at[which], inc=1, device_id=(o, q, r), device_id_type=MESH)
+
+    for peer, higher in beside_z:
+
+        @pl.when(jnp.logical_not(low | higher))
+        def _():
+            pl.semaphore_signal(ready.at[3], inc=1, device_id=peer, device_id_type=MESH)
 
     loads[0].wait()
 
@@ -180,6 +191,10 @@
             for k in range(2):
                 m = (2 * side + k) * cy
                 z_tx[side, k, at] = rows[m : m + cy]
+    @pl.when(jnp.logical_not(low) & (r < n_z - 1))
+    def _():
+        pl.semaphore_wait(ready.at[3], jnp.where(r == 0, 2, 1))
+
     for copy in push_z:
         copy.start()
 
@@ -481,7 +496,7 @@
             pltpu.SemaphoreType.DMA((10,)),
             pltpu.SemaphoreType.DMA((n_x,)),
             pltpu.SemaphoreType.DMA((n_x,)),
-            pltpu.SemaphoreType.REGULAR((3,)),
+            pltpu.SemaphoreType.REGULAR((4,)),
             pltpu.SemaphoreType.REGULAR,
             pltpu.VMEM((2, CAP, orb, orb), BF16),
             pltpu.SemaphoreType.REGULAR,

time: 54.4 us -> 54.3 us (level)
  no operation moved by 1% of the time
where the time goes in v5:
time: 54.3 us; the launch traced here: 54.1 us
  Pallas kernels  51.8 us (95%)
  local copies, waits for them, and re-layouts  2.29 us (4%)
    pallas_call x1, Pallas kernels, local(): pl.pallas_call(functools.partial(kernel, sizes), out_shape=jax.ShapeDtype...  51.8 us
    unnamed x5, local copies, waits for them, and re-layouts  2.29 us

profile of v5, /device:TPU:192, one launch (start us, length us, event | category | flops | bytes accessed | tf_op | source)
XLA Modules:
  0.0 54.1 jit_solution(3897092756505671173)
XLA Ops:
  0.0 0.0 copy-start.1
  0.0 0.7 %copy-done.1 = s32[1,1,1,7,1]{3,4,2,1,0:T(1,128)S(1)} copy-done((s32[1,1,1,7,1]{3,4,2,1,0:T(1,128)S(1)}, s32[1,1,1,7,1]{3,4,2,1,0:T(1,128)}, u32[]{:S(2)}) %copy-start.1) | copy-done | bytes 52
  0.7 0.0 copy-start
  0.7 0.8 %copy-done = f32[8,16,16]{2,1,0:T(8,128)S(1)} copy-done((f32[8,16,16]{2,1,0:T(8,128)S(1)}, f32[8,16,16]{2,1,0:T(8,128)}, u32[]{:S(2)}) %copy-start) | copy-done | bytes 8216
  1.5 51.8 %correction.1 = bf16[16,128,128]{2,1,0:T(8,128)(2,1)S(1)} custom-call(bf16[8,16,16,128]{3,2,1,0:T(8,128)(2,1)} %c_hbm.1, f32[8,16,16]{2,1,0:T(8,128)S(1)} %copy-done, s32[7]{0:T(128)S(1)} %bitcast.3), custom_call_target="tpu_custom_call" | custom-call | tf_op jit(solution)/shard_map/correction/pallas_call | solution.py:474
  53.3 0.8 %copy.5 = bf16[1,1,1,16,128,128]{5,4,3,2,1,0:T(8,128)(2,1)} copy(bf16[1,1,1,16,128,128]{5,4,3,2,1,0:T(8,128)(2,1)S(1)} %bitcast.2) | data formatting | bytes 1048576
Async XLA Ops:
  0.0 0.7 %copy-start.1 = (s32[1,1,1,7,1]{3,4,2,1,0:T(1,128)S(1)}, s32[1,1,1,7,1]{3,4,2,1,0:T(1,128)}, u32[]{:S(2)}) copy-start(s32[1,1,1,7,1]{3,4,2,1,0:T(1,128)} %param.5) | copy-start | bytes 88
  0.7 0.8 %copy-start = (f32[8,16,16]{2,1,0:T(8,128)S(1)}, f32[8,16,16]{2,1,0:T(8,128)}, u32[]{:S(2)}) copy-start(f32[8,16,16]{2,1,0:T(8,128)} %pot_hbm.1) | copy-start | bytes 24580
